TPU v7x, 32 devices: a whole 2x2x4 slice. The times are simulated.
32 devices in a mesh: row: 4 (over z), col: 8 (over y, x, core).
Axes of the slice: x: 2, y: 2, z: 4, core: 2. Of those that a mesh axis runs over, the one named last changes fastest.
Arguments:
- points_rhs: bfloat16 [262144, 16], P(('row', 'col')), may hold values from -6 to 6
- leaf_basis: bfloat16 [1024, 256, 64], P(('row', 'col')), may hold values from -0.375 to 0.375
- near_src: int32 [1024, 2], P(('row', 'col')), may hold values from -1 to 1023, as said below
- near_blocks: bfloat16 [1024, 2, 256, 256], P(('row', 'col')), may hold values from -0.25 to 0.25
- transfer_first: bfloat16 [1024, 64, 64], P(('row', 'col')), may hold values from -0.5 to 0.5
- transfer_second: bfloat16 [512, 64, 64], P(('row', 'col')), may hold values from -0.5 to 0.5
- transfer_third: bfloat16 [256, 64, 64], P(('row', 'col')), may hold values from -0.5 to 0.5
- far_zero: int32 [1024, 8], P(('row', 'col')), may hold values from -1 to 1023, as said below
- far_one: int32 [512, 8], P(('row', 'col')), may hold values from -1 to 511, as said below
- far_two: int32 [256, 8], P(('row', 'col')), may hold values from -1 to 255, as said below
- far_three: int32 [128, 8], P(('row', 'col')), may hold values from -1 to 127, as said below
- couple_zero: bfloat16 [1024, 8, 64, 64], P(('row', 'col')), may hold values from -0.25 to 0.25
- couple_one: bfloat16 [512, 8, 64, 64], P(('row', 'col')), may hold values from -0.25 to 0.25
- couple_two: bfloat16 [256, 8, 64, 64], P(('row', 'col')), may hold values from -0.25 to 0.25
- couple_three: bfloat16 [128, 8, 64, 64], P(('row', 'col')), may hold values from -0.25 to 0.25
Outputs:
- product: bfloat16 [262144, 16], P(('row', 'col'))
Inputs may be any that keep to these rules, and one draw needn't show every extreme that they name: `near_src`: each entry is -1 or a leaf whose index differs from its row's by at most 2; -1 only where that leaf would lie outside the grid. `far_zero`: each row has 7 or 8 live entries, first in the row; a live entry of leaf i lies in the same aligned block of 256 leaves as i. `far_one`: each row has 7 or 8 live entries, first in the row; a live entry of cluster i lies in the same aligned block of 128 clusters as i. `far_two`: each row has 7 or 8 live entries, first in the row; a live entry of cluster i lies in the same aligned block of 64 clusters as i. `far_three`: each row has 7 or 8 live entries, first in the row; live entries may name any cluster of the level.
All inputs are finite; a program needn't handle non-finite values.
Results may differ from a plain program's by a relative error of at most 0.0044.
Values may be sent and summed in bfloat16 or wider, within the bound.
No kernel may reach another device: no remote copies, remote signals or barrier semaphores. Data moves between devices by JAX's collectives and lax.ppermute only.
A program may use at most 128 MiB of HBM per device.

v0:
```python
import jax
import jax.numpy as jnp
from jax import lax
from jax.sharding import PartitionSpec as P

LEAF = 256
RANK = 64
NRHS = 16
TOP_LEVEL = lax.Precision.HIGHEST


def padded_2(cells, sides, width):
    for axis, dim in sides:
        count = lax.axis_size(axis)
        ends = count - 1
        head = lax.slice_in_dim(cells, 0, width, axis=dim)
        tail = lax.slice_in_dim(cells, cells.shape[dim] - width, cells.shape[dim], axis=dim)
        cells = jnp.concatenate(
            [
                lax.ppermute(tail, axis, [(i, (i + 1) % count) for i in range(ends)]),
                cells,
                lax.ppermute(head, axis, [((i + 1) % count, i) for i in range(ends)]),
            ],
            axis=dim,
        )
    return cells


def gather_active(table, local_ids, sources):
    is_live = sources >= 0
    selected_rows = jnp.take(table, jnp.clip(local_ids, 0, table.shape[0] - 1), axis=0)
    return jnp.where(is_live[:, :, None, None], selected_rows, jnp.zeros_like(selected_rows))


def couple_level(table, group_start, sources, coupling_block):
    selected_rows = gather_active(table, sources - group_start, sources)
    return jnp.einsum(
        "enyd,endc->eyc", coupling_block, selected_rows, preferred_element_type=jnp.float32
    )


def collect_group(skeleton):
    return lax.all_gather(skeleton, "col", axis=0, tiled=True)


def shards(
    points_rhs,
    leaf_basis,
    near_src,
    near_blocks,
    transfer_first,
    transfer_second,
    transfer_third,
    far_zero,
    far_one,
    far_two,
    far_three,
    couple_zero,
    couple_one,
    couple_two,
    couple_three,
):
    leaf_count = leaf_basis.shape[0]
    leaf_x = points_rhs.reshape(leaf_count, LEAF, NRHS)
    padded = padded_2(points_rhs.reshape(leaf_count, LEAF * NRHS), ((("row", "col"), 0),), 2)
    padded = padded.reshape(leaf_count + 4, LEAF, NRHS)
    skel_zero = jnp.einsum(
        "lpa,lpr->lar", leaf_basis, leaf_x, preferred_element_type=jnp.float32
    ).astype(jnp.bfloat16)
    skeletons = [skel_zero]
    transfers = [transfer_first, transfer_second, transfer_third]
    for transfer in transfers:
        child_skel = skeletons[-1]
        lifted = jnp.einsum(
            "cab,car->cbr", transfer, child_skel, preferred_element_type=jnp.float32
        )
        lifted = lifted.reshape(lifted.shape[0] // 2, 2, RANK, NRHS).sum(axis=1)
        skeletons.append(lifted.astype(jnp.bfloat16))
    tables = [collect_group(skeletons[level_index]) for level_index in range(3)]
    coarse_group = lax.all_gather(skeletons[3], "col", axis=0, tiled=True)
    coarse_table = lax.all_gather(coarse_group, "row", axis=0, tiled=True)
    row_index = lax.axis_index("row")
    lists = [far_zero, far_one, far_two]
    coupling_blocks = [couple_zero, couple_one, couple_two]
    coupled_field = []
    for level_index in range(3):
        group_start = row_index * tables[level_index].shape[0]
        coupled_field.append(
            couple_level(
                tables[level_index], group_start, lists[level_index], coupling_blocks[level_index]
            )
        )
    coupled_field.append(couple_level(coarse_table, 0, far_three, couple_three))
    downward_field = coupled_field[3]
    for level_index in (3, 2, 1):
        spread = jnp.repeat(downward_field, 2, axis=0)
        downward_field = coupled_field[level_index - 1] + jnp.einsum(
            "cab,cbr->car",
            transfers[level_index - 1].astype(jnp.float32),
            spread,
            precision=TOP_LEVEL,
        )
    far_out = jnp.einsum(
        "lpa,lar->lpr", leaf_basis.astype(jnp.float32), downward_field, precision=TOP_LEVEL
    )
    first_leaf = lax.axis_index(("row", "col")) * leaf_count
    near_picked = gather_active(padded, near_src - first_leaf + 2, near_src)
    near_out = jnp.einsum(
        "iknm,ikmr->inr", near_blocks, near_picked, preferred_element_type=jnp.float32
    )
    return (far_out + near_out).reshape(leaf_count * LEAF, NRHS).astype(jnp.bfloat16)


def solution(mesh):
    return jax.shard_map(
        shards,
        mesh=mesh,
        in_specs=(
            P(("row", "col"), None),
            P(("row", "col"), None, None),
            P(("row", "col"), None),
            P(("row", "col"), None, None, None),
            P(("row", "col"), None, None),
            P(("row", "col"), None, None),
            P(("row", "col"), None, None),
            P(("row", "col"), None),
            P(("row", "col"), None),
            P(("row", "col"), None),
            P(("row", "col"), None),
            P(("row", "col"), None, None, None),
            P(("row", "col"), None, None, None),
            P(("row", "col"), None, None, None),
            P(("row", "col"), None, None, None),
        ),
        out_specs=P(("row", "col"), None),
        check_vma=False,
    )
```

profile of v0, /device:TPU:0, one launch (start us, length us, event | category | flops | bytes accessed | tf_op | source)
XLA Modules:
  0.0 106.1 jit_solution(7011895499649475544)
XLA Ops:
  0.0 0.9 fusion.44
  1.0 0.8 slice.13
  1.8 3.0 %collective-permute-start = (bf16[2,4096]{1,0:T(2,128)(2,1)}, bf16[2,4096]{1,0:T(2,128)(2,1)}, u32[]{:S(2)}, u32[]{:S(2)}) collective-permute-start(bf16[2,4096]{1,0:T(2,128)(2,1)} %slice.13), channel_id=1, source_target_pairs={{0,1},{1,2},{2,3},{3,4},{4,5},{5,6},{6,7},{7,8},{8,9},{9,10},{10,1... | collective-permute-start | bytes 49160 | tf_op jit(solution)/shard_map/ppermute | solution.py:20
  4.9 0.8 slice.15
  5.7 1.3 %collective-permute-start.1 = (bf16[2,4096]{1,0:T(2,128)(2,1)}, bf16[2,4096]{1,0:T(2,128)(2,1)}, u32[]{:S(2)}, u32[]{:S(2)}) collective-permute-start(bf16[2,4096]{1,0:T(2,128)(2,1)} %slice.15), channel_id=1, source_target_pairs={{1,0},{2,1},{3,2},{4,3},{5,4},{6,5},{7,6},{8,7},{9,8},{10,9},{11,1... | collective-permute-start | bytes 49160 | tf_op jit(solution)/shard_map/ppermute | solution.py:22
  7.0 0.7 compare_select_fusion.3
  7.7 1.3 %broadcast_compare_fusion.3 = (pred[4,8]{1,0:T(4,128)(4,1)}, pred[4,8]{1,0:T(4,128)(4,1)}) fusion(s32[4,8]{1,0:T(4,128)} %param.25), kind=kLoop, calls=%fused_computation.72 | loop fusion | flops 256 | bytes 192 | tf_op jit(solution)/shard_map/ge | solution.py:30
  8.9 1.3 %compare_and_fusion = (pred[8,8]{1,0:T(8,128)(4,1)}, s32[8,8]{1,0:T(8,128)S(1)}, pred[8,8]{1,0:T(8,128)(4,1)}) fusion(s32[8,8]{1,0:T(8,128)} %param.24, s32[]{:T(128)S(6)} %mul.17), kind=kLoop, calls=%fused_computation.64 | loop fusion | flops 576 | bytes 644 | tf_op jit(solution)/shard_map/jit(_take)/and | solution.py:31
  10.3 1.6 %convolution_convert_fusion = bf16[32,64,16]{1,2,0:T(8,128)(2,1)S(1)} fusion(bf16[32,256,64]{1,2,0:T(8,128)(2,1)} %param.16, bf16[2,32,8,256]{3,2,1,0:T(8,128)(2,1)} %bitcast.75), kind=kOutput, calls=%fused_computation.11 | convolution fusion | flops 16809984 | bytes 1376256 | tf_op jit(solution)/shard_map/lpa,lpr->lar/dot_general | solution.py:67
  11.9 14.6 %all_gather.15 = bf16[256,64,16]{1,2,0:T(8,128)(2,1)S(1)} all-gather(bf16[32,64,16]{1,2,0:T(8,128)(2,1)S(1)} %convolution_convert_fusion), channel_id=1, replica_groups=mesh['row'=4,'col'=8] {'col'}, dimensions={0}, use_global_device_ids=true | all-gather | bytes 589824 | tf_op jit(solution)/shard_map/all_gather | solution.py:43
  26.6 1.3 %bitcast_reduce_fusion = bf16[16,64,16]{1,2,0:T(8,128)(2,1)S(1)} fusion(bf16[32,64,16]{1,2,0:T(8,128)(2,1)S(1)} %convolution_convert_fusion, bf16[32,64,64]{2,1,0:T(8,128)(2,1)} %param.19), kind=kOutput, calls=%fused_computation.35 | convolution fusion | flops 4210688 | bytes 360448 | tf_op jit(solution)/shard_map/cab,car->cbr/dot_general | solution.py:74
  27.9 10.0 %all_gather.16 = bf16[128,64,16]{1,2,0:T(8,128)(2,1)} all-gather(bf16[16,64,16]{1,2,0:T(8,128)(2,1)S(1)} %bitcast_reduce_fusion), channel_id=1, replica_groups=mesh['row'=4,'col'=8] {'col'}, dimensions={0}, use_global_device_ids=true | all-gather | bytes 294912 | tf_op jit(solution)/shard_map/all_gather | solution.py:43
  38.0 9.2 %all_gather.17 = bf16[64,64,16]{1,2,0:T(8,128)(2,1)S(1)} all-gather(bf16[8,64,16]{1,2,0:T(8,128)(2,1)S(1)} %bitcast_reduce_fusion.1), channel_id=1, replica_groups=mesh['row'=4,'col'=8] {'col'}, dimensions={0}, use_global_device_ids=true | all-gather | bytes 147456 | tf_op jit(solution)/shard_map/all_gather | solution.py:43
  47.4 8.3 %all_gather.18 = bf16[32,64,16]{1,2,0:T(8,128)(2,1)S(1)} all-gather(bf16[4,64,16]{1,2,0:T(8,128)(2,1)S(1)} %bitcast_reduce_fusion.2), channel_id=1, replica_groups=mesh['row'=4,'col'=8] {'col'}, dimensions={0}, use_global_device_ids=true | all-gather | bytes 73728 | tf_op jit(solution)/shard_map/all_gather | solution.py:80
  55.7 17.5 %all_gather.19 = bf16[128,64,16]{1,2,0:T(8,128)(2,1)} all-gather(bf16[32,64,16]{1,2,0:T(8,128)(2,1)S(1)} %all_gather.18), channel_id=1, replica_groups=mesh['row'=4,'col'=8] {'row'}, dimensions={0}, use_global_device_ids=true | all-gather | bytes 327680 | tf_op jit(solution)/shard_map/all_gather | solution.py:81
  74.1 0.7 copy.63
  75.8 1.3 %compare_and_fusion.3 = (pred[32,2]{0,1:T(4,128)(4,1)}, s32[32,2]{0,1:T(2,128)S(1)}, pred[32,2]{0,1:T(4,128)(4,1)}) fusion(s32[32,2]{0,1:T(2,128)} %param.17, s32[]{:T(128)S(6)} %mul.19), kind=kLoop, calls=%fused_computation.70 | loop fusion | flops 640 | bytes 644 | tf_op jit(solution)/shard_map/jit(_take)/and | solution.py:31
  77.1 0.7 reshape.102
  77.8 1.3 %gather_fusion.2 = bf16[64,64,16]{1,2,0:T(8,128)(2,1)} fusion(bf16[64,64,16]{1,2,0:T(8,128)(2,1)S(1)} %all_gather.17, s32[1024]{0:T(1024)S(1)} %pad_clamp_fusion.2), kind=kCustom, calls=%fused_computation.2 | custom fusion | bytes 262400 | tf_op jit(solution)/shard_map/jit(_take)/gather | solution.py:31
  79.1 1.6 %gather_fusion.3 = bf16[32,64,16]{1,2,0:T(8,128)(2,1)S(1)} fusion(bf16[128,64,16]{1,2,0:T(8,128)(2,1)} %all_gather.19, s32[1024]{0:T(1024)S(1)} %pad_clamp_fusion.1), kind=kCustom, calls=%fused_computation.3 | custom fusion | bytes 131200 | tf_op jit(solution)/shard_map/jit(_take)/gather | solution.py:31
  80.8 1.8 %convolution_bitcast_fusion.3 = f32[8,16,64]{2,1,0:T(8,128)S(1)} fusion(bf16[8,8,64,64]{3,2,1,0:T(8,128)(2,1)} %param.28, bf16[8,8,64,16]{2,3,1,0:T(8,128)(2,1)} %bitcast.73, pred[8,8]{1,0:T(8,128)(4,1)} %get-tuple-element.5, pred[8,8]{1,0:T(8,128)(4,1)} %get-tuple-element.15), kind=kOutput, calls=%fused_computation.17 | convolution fusion | flops 8519680 | bytes 688256 | tf_op jit(solution)/shard_map/enyd,endc->eyc/dot_general | solution.py:37
  82.5 1.4 %convolution_bitcast_fusion.4 = f32[4,64,16]{1,2,0:T(8,128)S(1)} fusion(bf16[4,8,64,64]{3,2,1,0:T(8,128)(2,1)} %param.29, bf16[4,8,64,16]{2,3,1,0:T(8,128)(2,1)S(1)} %bitcast.74, pred[4,8]{1,0:T(4,128)(4,1)} %get-tuple-element.19, pred[4,8]{1,0:T(4,128)(4,1)} %get-tuple-element.18), kind=kOutput, calls=%fused_computation.18 | convolution fusion | flops 4259840 | bytes 344128 | tf_op jit(solution)/shard_map/enyd,endc->eyc/dot_general | solution.py:37
  84.0 1.2 %fusion.3 = f32[8,64,16]{1,2,0:T(8,128)S(1)} fusion(f32[8,16,64]{2,1,0:T(8,128)S(1)} %convolution_bitcast_fusion.3, f32[8,64,16]{1,2,0:T(8,128)S(1)} %bitcast.80, bf16[8,64,64]{2,1,0:T(8,128)(2,1)} %param.21), kind=kOutput, calls=%fused_computation.16 | convolution fusion | flops 6299648 | bytes 163840 | tf_op jit(solution)/shard_map/cab,cbr->car/dot_general | solution.py:97
  85.2 2.5 %gather_fusion.1 = bf16[128,64,16]{1,2,0:T(8,128)(2,1)} fusion(bf16[128,64,16]{1,2,0:T(8,128)(2,1)} %all_gather.16, s32[1024]{0:T(1024)S(1)} %pad_clamp_fusion.3), kind=kCustom, calls=%fused_computation.1 | custom fusion | bytes 524800 | tf_op jit(solution)/shard_map/jit(_take)/gather | solution.py:31
  87.7 1.8 %convolution_bitcast_fusion.2 = f32[16,16,64]{2,1,0:T(8,128)S(1)} fusion(bf16[16,8,64,64]{3,2,1,0:T(8,128)(2,1)S(1)} %copy-done, bf16[16,8,64,16]{2,3,1,0:T(8,128)(2,1)} %bitcast.72, pred[16,8]{1,0:T(8,128)(4,1)} %copy.63, pred[16,8]{1,0:T(8,128)(4,1)S(1)} %copy-done.13), kind=kOutput, calls=%fused_computation.14 | convolution fusion | flops 17039360 | bytes 1376512 | tf_op jit(solution)/shard_map/enyd,endc->eyc/dot_general | solution.py:37
  90.0 1.8 %gather_fusion = bf16[256,64,16]{1,2,0:T(8,128)(2,1)} fusion(bf16[256,64,16]{1,2,0:T(8,128)(2,1)S(1)} %all_gather.15, s32[1024]{0:T(1024)S(1)} %pad_clamp_fusion.4), kind=kCustom, calls=%fused_computation | custom fusion | bytes 1049600 | tf_op jit(solution)/shard_map/jit(_take)/gather | solution.py:31
  91.8 3.3 %convolution_bitcast_fusion.1 = f32[32,16,64]{2,1,0:T(8,128)S(1)} fusion(bf16[32,8,64,64]{3,2,1,0:T(8,128)(2,1)} %param.26, bf16[32,8,64,16]{2,3,1,0:T(8,128)(2,1)} %bitcast.71, pred[32,8]{1,0:T(8,128)(4,1)S(1)} %copy-done.7, pred[32,8]{1,0:T(8,128)(4,1)S(1)} %copy.58), kind=kOutput, calls=%fused_computation.9 | convolution fusion | flops 34078720 | bytes 2753024 | tf_op jit(solution)/shard_map/enyd,endc->eyc/dot_general | solution.py:37
  95.2 0.9 convolution_add_fusion.1
  96.4 0.9 concatenate.8
  97.4 0.9 concatenate.9
  99.0 5.8 %convolution_bitcast_fusion = f32[32,16,256]{2,1,0:T(8,128)S(1)} fusion(bf16[32,2,256,256]{3,2,1,0:T(8,128)(2,1)} %param.18, bf16[32,2,256,16]{2,3,1,0:T(8,128)(2,1)S(1)} %bitcast.70, pred[32,2]{1,0:T(8,128)(4,1)S(1)} %copy.66, pred[32,2]{1,0:T(8,128)(4,1)S(1)} %copy.65), kind=kOutput, calls=%fused_computation.6 | convolution fusion | flops 134742016 | bytes 9437312 | tf_op jit(solution)/shard_map/iknm,ikmr->inr/dot_general | solution.py:108
  105.4 0.7 copy.80
  (63 shorter events, 4.9 us)
Async XLA Ops:
  0.0 87.7 %copy-start = (bf16[16,8,64,64]{3,2,1,0:T(8,128)(2,1)S(1)}, bf16[16,8,64,64]{3,2,1,0:T(8,128)(2,1)}, u32[]{:S(2)}) copy-start(bf16[16,8,64,64]{3,2,1,0:T(8,128)(2,1)} %param.27) | copy-start | bytes 3145732
  0.0 37.8 %copy-start.4 = (bf16[16,64,64]{2,1,0:T(8,128)(2,1)S(1)}, bf16[16,64,64]{2,1,0:T(8,128)(2,1)}, u32[]{:S(2)}) copy-start(bf16[16,64,64]{2,1,0:T(8,128)(2,1)} %param.20) | copy-start | bytes 393220
  0.0 47.2 %copy-start.6 = (bf16[8,64,64]{2,1,0:T(8,128)(2,1)S(1)}, bf16[8,64,64]{2,1,0:T(8,128)(2,1)}, u32[]{:S(2)}) copy-start(bf16[8,64,64]{2,1,0:T(8,128)(2,1)} %param.21) | copy-start | bytes 196612
  0.0 73.3 %copy-start.8 = (s32[16,8]{0,1:T(8,128)S(1)}, s32[16,8]{0,1:T(8,128)}, u32[]{:S(2)}) copy-start(s32[16,8]{0,1:T(8,128)} %param.23) | copy-start | bytes 1540
  0.0 74.8 %copy-start.9 = (s32[32,8]{0,1:T(8,128)S(1)}, s32[32,8]{0,1:T(8,128)}, u32[]{:S(2)}) copy-start(s32[32,8]{0,1:T(8,128)} %param.22) | copy-start | bytes 3076
  1.8 94.6 %collective-permute-start = (bf16[2,4096]{1,0:T(2,128)(2,1)}, bf16[2,4096]{1,0:T(2,128)(2,1)}, u32[]{:S(2)}, u32[]{:S(2)}) collective-permute-start(bf16[2,4096]{1,0:T(2,128)(2,1)} %slice.13), channel_id=1, source_target_pairs={{0,1},{1,2},{2,3},{3,4},{4,5},{5,6},{6,7},{7,8},{8,9},{9,10},{10,1... | collective-permute-start | bytes 49160 | tf_op jit(solution)/shard_map/ppermute | solution.py:20
  5.7 91.7 %collective-permute-start.1 = (bf16[2,4096]{1,0:T(2,128)(2,1)}, bf16[2,4096]{1,0:T(2,128)(2,1)}, u32[]{:S(2)}, u32[]{:S(2)}) collective-permute-start(bf16[2,4096]{1,0:T(2,128)(2,1)} %slice.15), channel_id=1, source_target_pairs={{1,0},{2,1},{3,2},{4,3},{5,4},{6,5},{7,6},{8,7},{9,8},{10,9},{11,1... | collective-permute-start | bytes 49160 | tf_op jit(solution)/shard_map/ppermute | solution.py:22
  79.1 8.6 %copy-start.13 = (pred[16,8]{1,0:T(8,128)(4,1)S(1)}, pred[16,8]{1,0:T(8,128)(4,1)}, u32[]{:S(2)}) copy-start(pred[16,8]{1,0:T(8,128)(4,1)} %copy.62) | copy-start | bytes 388
  82.5 7.0 %copy-start.5 = (bf16[16,64,64]{2,1,0:T(8,128)(2,1)S(1)}, bf16[16,64,64]{2,1,0:T(8,128)(2,1)}, u32[]{:S(2)}) copy-start(bf16[16,64,64]{2,1,0:T(8,128)(2,1)} %param.20) | copy-start | bytes 393220
  90.0 1.8 %copy-start.7 = (pred[32,8]{1,0:T(8,128)(4,1)S(1)}, pred[32,8]{1,0:T(8,128)(4,1)}, u32[]{:S(2)}) copy-start(pred[32,8]{1,0:T(8,128)(4,1)} %copy.59) | copy-start | bytes 772
  91.8 3.4 %copy-start.2 = (bf16[32,64,64]{2,1,0:T(8,128)(2,1)S(1)}, bf16[32,64,64]{2,1,0:T(8,128)(2,1)}, u32[]{:S(2)}) copy-start(bf16[32,64,64]{2,1,0:T(8,128)(2,1)} %param.19) | copy-start | bytes 786436
  91.8 4.4 %copy-start.12 = (s32[64]{0:T(128)S(1)}, s32[64]{0:T(128)}, u32[]{:S(2)}) copy-start(s32[64]{0:T(128)} %reshape.102) | copy-start | bytes 772
  91.8 4.4 %copy-start.3 = (bf16[8192,16]{0,1:T(8,128)(2,1)S(1)}, bf16[8192,16]{0,1:T(8,128)(2,1)}, u32[]{:S(2)}) copy-start(bf16[8192,16]{0,1:T(8,128)(2,1)} %param.15) | copy-start | bytes 786436
  91.8 4.4 %copy-start.11 = (pred[32,2]{0,1:T(4,128)(4,1)S(1)}, pred[32,2]{0,1:T(4,128)(4,1)}, u32[]{:S(2)}) copy-start(pred[32,2]{0,1:T(4,128)(4,1)} %get-tuple-element.20) | copy-start | bytes 196
  91.8 4.5 %copy-start.10 = (pred[32,2]{0,1:T(4,128)(4,1)S(1)}, pred[32,2]{0,1:T(4,128)(4,1)}, u32[]{:S(2)}) copy-start(pred[32,2]{0,1:T(4,128)(4,1)} %get-tuple-element.11) | copy-start | bytes 196
  99.0 5.8 %copy-start.1 = (bf16[32,256,64]{1,2,0:T(8,128)(2,1)S(1)}, bf16[32,256,64]{1,2,0:T(8,128)(2,1)}, u32[]{:S(2)}) copy-start(bf16[32,256,64]{1,2,0:T(8,128)(2,1)} %param.16) | copy-start | bytes 3145732
where the time goes:
time: 107 us; the launch traced here: 106 us
  blocking collectives  59.6 us (56%)
  matrix products  20.5 us (19%)
  local copies, waits for them, and re-layouts  16.8 us (16%)
  other arithmetic  4.61 us (4%)
  starting transfers between devices  4.27 us (4%)
    all_gather x3, blocking collectives, collect_group(): return lax.all_gather(skeleton, 'col', axis=0, tiled=True)  33.8 us
    all_gather x1, blocking collectives, shards(): coarse_table = lax.all_gather(coarse_group, 'row', axis=0, tiled=True)  17.5 us
    all_gather x1, blocking collectives, shards(): coarse_group = lax.all_gather(skeletons[3], 'col', axis=0, tiled=True)  8.34 us
    dot_general x4, matrix products, couple_level(): jnp.einsum('enyd,endc->eyc', coupling_block, selected_rows, preferred_ele...  8.29 us
    gather x5, local copies, waits for them, and re-layouts, gather_active(): jnp.take(table, jnp.clip(local_ids, 0, table.shape[0] - 1), axis=0)  7.86 us
    dot_general x1, matrix products, shards(): jnp.einsum('iknm,ikmr->inr', near_blocks, near_picked, preferred_element_...  5.76 us
    ppermute x1, starting transfers between devices, padded_2(): lax.ppermute(tail, axis, [(i, (i + 1) % count) for i in range(ends)])  2.99 us
    dot_general x3, matrix products, shards(): jnp.einsum('cab,cbr->car', transfers[level_index - 1].astype(jnp.float32)...  2.64 us
  transfers between devices with their start and end apart: 2, of which 0 were waited for; matrix products, arithmetic and copies ran while one was open for 30% of the time, Pallas kernels for 0%

commit v1 on v0

--- a/solution.py
+++ b/solution.py
@@ -78,7 +78,14 @@
         skeletons.append(lifted.astype(jnp.bfloat16))
     tables = [collect_group(skeletons[level_index]) for level_index in range(3)]
     coarse_group = lax.all_gather(skeletons[3], "col", axis=0, tiled=True)
-    coarse_table = lax.all_gather(coarse_group, "row", axis=0, tiled=True)
+    peers = lax.axis_size("row")
+    forward = [(i_2, (i_2 + 1) % peers) for i_2 in range(peers)]
+    shards_2 = [coarse_group]
+    for hop in range(1, peers):
+        shards_2 = [lax.ppermute(shards_2[0], "row", forward), *shards_2]
+    full = jnp.concatenate(shards_2, axis=0)
+    shift = (lax.axis_index("row") + 1) * shards_2[-1].shape[0]
+    coarse_table = jnp.roll(full, shift, axis=0)
     row_index = lax.axis_index("row")
     lists = [far_zero, far_one, far_two]
     coupling_blocks = [couple_zero, couple_one, couple_two]

time: 107 us -> 119 us (1.11)
  blocking collectives: 59.6 us -> 43.6 us
  local copies, waits for them, and re-layouts: 16.8 us -> 24.5 us
  matrix products: 20.5 us -> 28.1 us
  waiting for transfers between devices: 0.01 us -> 4.68 us
  starting transfers between devices: 4.27 us -> 8.58 us
  other arithmetic: 4.61 us -> 8.13 us
    all_gather x1 -> x0, blocking collectives: 17.5 us -> none  [shards(): coarse_table = lax.all_gather(coarse_group, 'row', axis=0, tiled=True)]
    ppermute x0 -> x3, starting transfers between devices: none -> 4.74 us  [shards(): shards_2 = [lax.ppermute(shards_2[0], 'row', forward), *shards_2]]
    ppermute x0 -> x3, waiting for transfers between devices: none -> 4.67 us  [shards(): shards_2 = [lax.ppermute(shards_2[0], 'row', forward), *shards_2]]
    gather x5, other arithmetic: 0.04 us -> 2.48 us  [gather_active(): jnp.take(table, jnp.clip(local_ids, 0, table.shape[0] - 1), axis=0)]
    all_gather x1, blocking collectives: 8.34 us -> 10.7 us  [shards(): coarse_group = lax.all_gather(skeletons[3], 'col', axis=0, tiled=True)]
    unnamed x28 -> x39, local copies, waits for them, and re-layouts: 0.06 us -> 2.1 us
    dot_general x3, matrix products: 2.64 us -> 4.66 us  [shards(): jnp.einsum('cab,cbr->car', transfers[level_index - 1].astype(jnp.float32)...]
    dot_general x3, matrix products: 1.63 us -> 3.54 us  [shards(): jnp.einsum('cab,car->cbr', transfer, child_skel, preferred_element_type=j...]
  transfers between devices with their start and end apart: 2 -> 5, of which waited for: 0 -> 1; matrix products, arithmetic and copies ran while one was open for 30% -> 36% of each run, Pallas kernels for 0% -> 0%
where the time goes in v1:
time: 119 us; the launch traced here: 118 us
  blocking collectives  43.6 us (37%)
  matrix products  28.1 us (24%)
  local copies, waits for them, and re-layouts  24.5 us (21%)
  starting transfers between devices  8.58 us (7%)
  other arithmetic  8.13 us (7%)
  waiting for transfers between devices  4.68 us (4%)
    all_gather x3, blocking collectives, collect_group(): return lax.all_gather(skeleton, 'col', axis=0, tiled=True)  32.9 us
    all_gather x1, blocking collectives, shards(): coarse_group = lax.all_gather(skeletons[3], 'col', axis=0, tiled=True)  10.7 us
    dot_general x4, matrix products, couple_level(): jnp.einsum('enyd,endc->eyc', coupling_block, selected_rows, preferred_ele...  9.98 us
    gather x5, local copies, waits for them, and re-layouts, gather_active(): jnp.take(table, jnp.clip(local_ids, 0, table.shape[0] - 1), axis=0)  8.1 us
    dot_general x1, matrix products, shards(): jnp.einsum('iknm,ikmr->inr', near_blocks, near_picked, preferred_element_...  6.49 us
    ppermute x3, starting transfers between devices, shards(): shards_2 = [lax.ppermute(shards_2[0], 'row', forward), *shards_2]  4.74 us
    ppermute x3, waiting for transfers between devices, shards(): shards_2 = [lax.ppermute(shards_2[0], 'row', forward), *shards_2]  4.67 us
    dot_general x3, matrix products, shards(): jnp.einsum('cab,cbr->car', transfers[level_index - 1].astype(jnp.float32)...  4.66 us
  transfers between devices with their start and end apart: 5, of which 1 were waited for; matrix products, arithmetic and copies ran while one was open for 36% of the time, Pallas kernels for 0%

profile of v1, /device:TPU:0, one launch (start us, length us, event | category | flops | bytes accessed | tf_op | source)
XLA Modules:
  0.0 117.9 jit_solution(16793975363139926753)
XLA Ops:
  0.0 1.8 %convolution_convert_fusion = bf16[32,64,16]{1,2,0:T(8,128)(2,1)S(1)} fusion(bf16[32,256,64]{1,2,0:T(8,128)(2,1)} %param.16, bf16[2,32,8,256]{3,2,1,0:T(8,128)(2,1)} %bitcast.75), kind=kOutput, calls=%fused_computation.11 | convolution fusion | flops 16809984 | bytes 1376256 | tf_op jit(solution)/shard_map/lpa,lpr->lar/dot_general | solution.py:67
  1.8 1.4 %bitcast_reduce_fusion = bf16[16,64,16]{1,2,0:T(8,128)(2,1)S(1)} fusion(bf16[32,64,16]{1,2,0:T(8,128)(2,1)S(1)} %convolution_convert_fusion, bf16[32,64,64]{2,1,0:T(8,128)(2,1)} %param.19), kind=kOutput, calls=%fused_computation.35 | convolution fusion | flops 4210688 | bytes 360448 | tf_op jit(solution)/shard_map/cab,car->cbr/dot_general | solution.py:74
  3.2 1.1 bitcast_reduce_fusion.1
  4.3 1.1 bitcast_reduce_fusion.2
  5.4 10.7 %all_gather.15 = bf16[32,64,16]{1,2,0:T(8,128)(2,1)S(1)} all-gather(bf16[4,64,16]{1,2,0:T(8,128)(2,1)S(1)} %bitcast_reduce_fusion.2), channel_id=1, replica_groups=mesh['row'=4,'col'=8] {'col'}, dimensions={0}, use_global_device_ids=true | all-gather | bytes 73728 | tf_op jit(solution)/shard_map/all_gather | solution.py:80
  16.1 1.6 %collective-permute-start = (bf16[32,64,16]{1,2,0:T(8,128)(2,1)S(1)}, bf16[32,64,16]{1,2,0:T(8,128)(2,1)}, u32[]{:S(2)}, u32[]{:S(2)}) collective-permute-start(bf16[32,64,16]{1,2,0:T(8,128)(2,1)S(1)} %all_gather.15), channel_id=1, source_target_pairs={{0,8},{8,16},{16,24},{24,0},{1,9},{9,17},{17,25},{25,1},{2,10},{10... | collective-permute-start | bytes 196616 | tf_op jit(solution)/shard_map/ppermute | solution.py:85
  19.3 2.6 %collective-permute-start.3 = (bf16[2,4096]{1,0:T(2,128)(2,1)}, bf16[2,4096]{1,0:T(2,128)(2,1)}, u32[]{:S(2)}, u32[]{:S(2)}) collective-permute-start(bf16[2,4096]{1,0:T(2,128)(2,1)} %slice.13), channel_id=1, source_target_pairs={{0,1},{1,2},{2,3},{3,4},{4,5},{5,6},{6,7},{7,8},{8,9},{9,10},{10,1... | collective-permute-start | bytes 49160 | tf_op jit(solution)/shard_map/ppermute | solution.py:20
  22.7 1.3 %collective-permute-start.4 = (bf16[2,4096]{1,0:T(2,128)(2,1)}, bf16[2,4096]{1,0:T(2,128)(2,1)}, u32[]{:S(2)}, u32[]{:S(2)}) collective-permute-start(bf16[2,4096]{1,0:T(2,128)(2,1)} %slice.15), channel_id=1, source_target_pairs={{1,0},{2,1},{3,2},{4,3},{5,4},{6,5},{7,6},{8,7},{9,8},{10,9},{11,1... | collective-permute-start | bytes 49160 | tf_op jit(solution)/shard_map/ppermute | solution.py:22
  24.7 1.2 %broadcast_compare_fusion.3 = (pred[4,8]{1,0:T(4,128)(4,1)}, pred[4,8]{1,0:T(4,128)(4,1)}) fusion(s32[4,8]{1,0:T(4,128)} %param.25), kind=kLoop, calls=%fused_computation.80 | loop fusion | flops 256 | bytes 192 | tf_op jit(solution)/shard_map/ge | solution.py:30
  25.9 11.9 %all_gather.14 = bf16[64,64,16]{1,2,0:T(8,128)(2,1)S(1)} all-gather(bf16[8,64,16]{1,2,0:T(8,128)(2,1)S(1)} %bitcast_reduce_fusion.1), channel_id=1, replica_groups=mesh['row'=4,'col'=8] {'col'}, dimensions={0}, use_global_device_ids=true | all-gather | bytes 147456 | tf_op jit(solution)/shard_map/all_gather | solution.py:43
  37.8 9.9 %all_gather.13 = bf16[128,64,16]{1,2,0:T(8,128)(2,1)} all-gather(bf16[16,64,16]{1,2,0:T(8,128)(2,1)S(1)} %bitcast_reduce_fusion), channel_id=1, replica_groups=mesh['row'=4,'col'=8] {'col'}, dimensions={0}, use_global_device_ids=true | all-gather | bytes 294912 | tf_op jit(solution)/shard_map/all_gather | solution.py:43
  47.7 11.1 %all_gather.12 = bf16[256,64,16]{1,2,0:T(8,128)(2,1)S(1)} all-gather(bf16[32,64,16]{1,2,0:T(8,128)(2,1)} %copy-done.5), channel_id=1, replica_groups=mesh['row'=4,'col'=8] {'col'}, dimensions={0}, use_global_device_ids=true | all-gather | bytes 589824 | tf_op jit(solution)/shard_map/all_gather | solution.py:43
  62.1 1.3 %copy.62 = pred[16,8]{1,0:T(8,128)(4,1)} copy(pred[16,8]{0,1:T(8,128)(4,1)} %get-tuple-element.16) | data formatting | bytes 256 | tf_op jit(solution)/shard_map/ge | solution.py:30
  63.5 1.3 %copy.63 = pred[16,8]{1,0:T(8,128)(4,1)} copy(pred[16,8]{0,1:T(8,128)(4,1)} %get-tuple-element.7) | data formatting | bytes 256 | tf_op jit(solution)/shard_map/jit(_take)/and | solution.py:31
  64.8 1.3 %compare_and_fusion.2 = (pred[32,8]{0,1:T(8,128)(4,1)}, s32[32,8]{0,1:T(8,128)}, pred[32,8]{0,1:T(8,128)(4,1)}) fusion(s32[32,8]{0,1:T(8,128)} %param.22, s32[]{:T(128)S(6)} %mul.18), kind=kLoop, calls=%fused_computation.74 | loop fusion | flops 2304 | bytes 2564 | tf_op jit(solution)/shard_map/jit(_take)/and | solution.py:31
  69.7 1.2 %compare_and_fusion.3 = (pred[32,2]{0,1:T(4,128)(4,1)}, s32[32,2]{0,1:T(2,128)S(1)}, pred[32,2]{0,1:T(4,128)(4,1)}) fusion(s32[32,2]{0,1:T(2,128)} %param.17, s32[]{:T(128)S(6)} %mul.23), kind=kLoop, calls=%fused_computation.78 | loop fusion | flops 640 | bytes 644 | tf_op jit(solution)/shard_map/jit(_take)/and | solution.py:31
  71.6 1.4 %reshape.102 = s32[64]{0:T(128)} reshape(s32[32,2]{1,0:T(8,128)} %copy.72) | data formatting | bytes 512 | tf_op jit(solution)/shard_map/jit(_take)/broadcast_in_dim | solution.py:31
  73.1 1.4 %gather_fusion.2 = bf16[64,64,16]{1,2,0:T(8,128)(2,1)} fusion(bf16[64,64,16]{1,2,0:T(8,128)(2,1)S(1)} %all_gather.14, s32[1024]{0:T(1024)} %pad_clamp_fusion.2), kind=kCustom, calls=%fused_computation.2 | custom fusion | bytes 262400 | tf_op jit(solution)/shard_map/jit(_take)/gather | solution.py:31
  74.5 2.7 %gather_fusion.1 = bf16[128,64,16]{1,2,0:T(8,128)(2,1)} fusion(bf16[128,64,16]{1,2,0:T(8,128)(2,1)} %all_gather.13, s32[1024]{0:T(1024)} %pad_clamp_fusion.3), kind=kCustom, calls=%fused_computation.1 | custom fusion | bytes 524800 | tf_op jit(solution)/shard_map/jit(_take)/gather | solution.py:31
  77.2 1.8 %gather_fusion = bf16[256,64,16]{1,2,0:T(8,128)(2,1)} fusion(bf16[256,64,16]{1,2,0:T(8,128)(2,1)S(1)} %all_gather.12, s32[1024]{0:T(1024)S(1)} %pad_clamp_fusion.4), kind=kCustom, calls=%fused_computation | custom fusion | bytes 1049600 | tf_op jit(solution)/shard_map/jit(_take)/gather | solution.py:31
  78.9 2.4 %convolution_bitcast_fusion.3 = f32[8,16,64]{2,1,0:T(8,128)} fusion(bf16[8,8,64,64]{3,2,1,0:T(8,128)(2,1)} %param.28, bf16[8,8,64,16]{2,3,1,0:T(8,128)(2,1)S(1)} %bitcast.73, pred[8,8]{1,0:T(8,128)(4,1)S(1)} %copy-done.13, pred[8,8]{1,0:T(8,128)(4,1)} %get-tuple-element.15), kind=kOutput, calls=%fused_computation.17 | convolution fusion | flops 8519680 | bytes 688256 | tf_op jit(solution)/shard_map/enyd,endc->eyc/dot_general | solution.py:37
  81.4 2.5 %convolution_bitcast_fusion.2 = f32[16,16,64]{2,1,0:T(8,128)} fusion(bf16[16,8,64,64]{3,2,1,0:T(8,128)(2,1)S(1)} %copy-done, bf16[16,8,64,16]{2,3,1,0:T(8,128)(2,1)} %bitcast.72, pred[16,8]{1,0:T(8,128)(4,1)} %copy.63, pred[16,8]{1,0:T(8,128)(4,1)} %copy.62), kind=kOutput, calls=%fused_computation.14 | convolution fusion | flops 17039360 | bytes 1376512 | tf_op jit(solution)/shard_map/enyd,endc->eyc/dot_general | solution.py:37
  83.8 3.8 %convolution_bitcast_fusion.1 = f32[32,16,64]{2,1,0:T(8,128)} fusion(bf16[32,8,64,64]{3,2,1,0:T(8,128)(2,1)} %param.26, bf16[32,8,64,16]{2,3,1,0:T(8,128)(2,1)S(1)} %bitcast.71, pred[32,8]{1,0:T(8,128)(4,1)S(1)} %copy.59, pred[32,8]{1,0:T(8,128)(4,1)S(1)} %copy.58), kind=kOutput, calls=%fused_computation.9 | convolution fusion | flops 34078720 | bytes 2753024 | tf_op jit(solution)/shard_map/enyd,endc->eyc/dot_general | solution.py:37
  89.8 2.5 %collective-permute-start.1 = (bf16[32,64,16]{1,2,0:T(8,128)(2,1)}, bf16[32,64,16]{1,2,0:T(8,128)(2,1)S(1)}, u32[]{:S(2)}, u32[]{:S(2)}) collective-permute-start(bf16[32,64,16]{1,2,0:T(8,128)(2,1)} %collective-permute-done), channel_id=1, source_target_pairs={{0,8},{8,16},{16,24},{24,0},{1,9},{9,17},{17,25},{25,1},{2,10},{10... | collective-permute-start | bytes 196616 | tf_op jit(solution)/shard_map/ppermute | solution.py:85
  93.0 4.7 %collective-permute-done.1 = bf16[32,64,16]{1,2,0:T(8,128)(2,1)S(1)} collective-permute-done((bf16[32,64,16]{1,2,0:T(8,128)(2,1)}, bf16[32,64,16]{1,2,0:T(8,128)(2,1)S(1)}, u32[]{:S(2)}, u32[]{:S(2)}) %collective-permute-start.1) | collective-permute-done | bytes 65568 | tf_op jit(solution)/shard_map/ppermute | solution.py:85
  98.3 6.5 %convolution_bitcast_fusion = f32[32,16,256]{2,1,0:T(8,128)} fusion(bf16[32,2,256,256]{3,2,1,0:T(8,128)(2,1)} %param.18, bf16[32,2,256,16]{2,3,1,0:T(8,128)(2,1)S(1)} %bitcast.70, pred[32,2]{1,0:T(8,128)(4,1)S(1)} %copy.66, pred[32,2]{1,0:T(8,128)(4,1)S(1)} %copy.65), kind=kOutput, calls=%fused_computation.6 | convolution fusion | flops 134742016 | bytes 9437312 | tf_op jit(solution)/shard_map/iknm,ikmr->inr/dot_general | solution.py:115
  107.8 1.6 %gather_fusion.3 = bf16[32,64,16]{1,2,0:T(8,128)(2,1)S(1)} fusion(bf16[128,64,16]{1,2,0:T(8,128)(2,1)} %constant_dynamic-slice_fusion, s32[1024]{0:T(1024)S(1)} %copy-done.7), kind=kCustom, calls=%fused_computation.3 | custom fusion | bytes 131200 | tf_op jit(solution)/shard_map/jit(_take)/gather | solution.py:31
  109.4 1.3 %convolution_bitcast_fusion.4 = f32[4,64,16]{1,2,0:T(8,128)S(1)} fusion(bf16[4,8,64,64]{3,2,1,0:T(8,128)(2,1)} %param.29, bf16[4,8,64,16]{2,3,1,0:T(8,128)(2,1)S(1)} %bitcast.74, pred[4,8]{1,0:T(4,128)(4,1)S(1)} %copy-done.15, pred[4,8]{1,0:T(4,128)(4,1)S(1)} %copy-done.14), kind=kOutput, calls=%fused_computation.18 | convolution fusion | flops 4259840 | bytes 344128 | tf_op jit(solution)/shard_map/enyd,endc->eyc/dot_general | solution.py:37
  110.8 1.1 fusion.3
  112.0 1.5 %fusion.2 = f32[16,64,16]{1,2,0:T(8,128)S(1)} fusion(f32[16,16,64]{2,1,0:T(8,128)} %convolution_bitcast_fusion.2, f32[16,64,16]{1,2,0:T(8,128)S(1)} %bitcast.79, bf16[16,64,64]{2,1,0:T(8,128)(2,1)} %param.20), kind=kOutput, calls=%fused_computation.13 | convolution fusion | flops 12599296 | bytes 327680 | tf_op jit(solution)/shard_map/cab,cbr->car/dot_general | solution.py:104
  113.5 2.0 %convolution_add_fusion.1 = f32[32,16,64]{2,1,0:T(8,128)S(1)} fusion(f32[32,16,64]{2,1,0:T(8,128)} %convolution_bitcast_fusion.1, f32[32,64,16]{1,2,0:T(8,128)S(1)} %bitcast.77, bf16[32,64,64]{2,1,0:T(8,128)(2,1)} %param.19), kind=kOutput, calls=%fused_computation.8 | convolution fusion | flops 25198592 | bytes 655360 | tf_op jit(solution)/shard_map/cab,cbr->car/dot_general | solution.py:104
  115.5 1.6 %fusion.1 = bf16[32,2,8,256]{3,2,1,0:T(8,128)(2,1)S(1)} fusion(f32[32,16,256]{2,1,0:T(8,128)} %convolution_bitcast_fusion, f32[32,16,64]{2,1,0:T(8,128)S(1)} %convolution_add_fusion.1, bf16[32,256,64]{1,2,0:T(8,128)(2,1)S(1)} %copy-done.2), kind=kOutput, calls=%fused_computation.10 | convolution fusion | flops 100925440 | bytes 1966080 | tf_op jit(solution)/shard_map/lpa,lar->lpr/dot_general | solution.py:110
  (81 shorter events, 18.0 us)
Async XLA Ops:
  0.0 81.3 %copy-start = (bf16[16,8,64,64]{3,2,1,0:T(8,128)(2,1)S(1)}, bf16[16,8,64,64]{3,2,1,0:T(8,128)(2,1)}, u32[]{:S(2)}) copy-start(bf16[16,8,64,64]{3,2,1,0:T(8,128)(2,1)} %param.27) | copy-start | bytes 3145732
  0.0 59.5 %copy-start.8 = (s32[8,8]{1,0:T(8,128)S(1)}, s32[8,8]{1,0:T(8,128)}, u32[]{:S(2)}) copy-start(s32[8,8]{1,0:T(8,128)} %param.24) | copy-start | bytes 772
  0.0 60.8 %copy-start.9 = (s32[16,8]{0,1:T(8,128)S(1)}, s32[16,8]{0,1:T(8,128)}, u32[]{:S(2)}) copy-start(s32[16,8]{0,1:T(8,128)} %param.23) | copy-start | bytes 1540
  1.8 3.6 %copy-start.5 = (bf16[32,64,16]{1,2,0:T(8,128)(2,1)}, bf16[32,64,16]{1,2,0:T(8,128)(2,1)S(1)}, u32[]{:S(2)}) copy-start(bf16[32,64,16]{1,2,0:T(8,128)(2,1)S(1)} %convolution_convert_fusion) | copy-start | bytes 196612
  16.1 73.7 %collective-permute-start = (bf16[32,64,16]{1,2,0:T(8,128)(2,1)S(1)}, bf16[32,64,16]{1,2,0:T(8,128)(2,1)}, u32[]{:S(2)}, u32[]{:S(2)}) collective-permute-start(bf16[32,64,16]{1,2,0:T(8,128)(2,1)S(1)} %all_gather.15), channel_id=1, source_target_pairs={{0,8},{8,16},{16,24},{24,0},{1,9},{9,17},{17,25},{25,1},{2,10},{10... | collective-permute-start | bytes 196616 | tf_op jit(solution)/shard_map/ppermute | solution.py:85
  19.3 68.6 %collective-permute-start.3 = (bf16[2,4096]{1,0:T(2,128)(2,1)}, bf16[2,4096]{1,0:T(2,128)(2,1)}, u32[]{:S(2)}, u32[]{:S(2)}) collective-permute-start(bf16[2,4096]{1,0:T(2,128)(2,1)} %slice.13), channel_id=1, source_target_pairs={{0,1},{1,2},{2,3},{3,4},{4,5},{5,6},{6,7},{7,8},{8,9},{9,10},{10,1... | collective-permute-start | bytes 49160 | tf_op jit(solution)/shard_map/ppermute | solution.py:20
  22.7 66.1 %collective-permute-start.4 = (bf16[2,4096]{1,0:T(2,128)(2,1)}, bf16[2,4096]{1,0:T(2,128)(2,1)}, u32[]{:S(2)}, u32[]{:S(2)}) collective-permute-start(bf16[2,4096]{1,0:T(2,128)(2,1)} %slice.15), channel_id=1, source_target_pairs={{1,0},{2,1},{3,2},{4,3},{5,4},{6,5},{7,6},{8,7},{9,8},{10,9},{11,1... | collective-permute-start | bytes 49160 | tf_op jit(solution)/shard_map/ppermute | solution.py:22
  77.2 1.8 %copy-start.3 = (bf16[64,64,16]{1,2,0:T(8,128)(2,1)S(1)}, bf16[64,64,16]{1,2,0:T(8,128)(2,1)}, u32[]{:S(2)}) copy-start(bf16[64,64,16]{1,2,0:T(8,128)(2,1)} %gather_fusion.2) | copy-start | bytes 393220
  77.2 1.8 %copy-start.13 = (pred[8,8]{1,0:T(8,128)(4,1)S(1)}, pred[8,8]{1,0:T(8,128)(4,1)}, u32[]{:S(2)}) copy-start(pred[8,8]{1,0:T(8,128)(4,1)} %get-tuple-element.5) | copy-start | bytes 196
  78.9 4.9 %copy-start.1 = (bf16[256,64,16]{1,2,0:T(8,128)(2,1)S(1)}, bf16[256,64,16]{1,2,0:T(8,128)(2,1)}, u32[]{:S(2)}) copy-start(bf16[256,64,16]{1,2,0:T(8,128)(2,1)} %gather_fusion) | copy-start | bytes 1572868
  81.3 6.3 %copy-start.12 = (s32[64]{0:T(128)S(1)}, s32[64]{0:T(128)}, u32[]{:S(2)}) copy-start(s32[64]{0:T(128)} %reshape.102) | copy-start | bytes 772
  81.3 6.3 %copy-start.4 = (bf16[8192,16]{0,1:T(8,128)(2,1)S(1)}, bf16[8192,16]{0,1:T(8,128)(2,1)}, u32[]{:S(2)}) copy-start(bf16[8192,16]{0,1:T(8,128)(2,1)} %param.15) | copy-start | bytes 786436
  81.4 6.3 %copy-start.11 = (pred[32,2]{0,1:T(4,128)(4,1)S(1)}, pred[32,2]{0,1:T(4,128)(4,1)}, u32[]{:S(2)}) copy-start(pred[32,2]{0,1:T(4,128)(4,1)} %get-tuple-element.20) | copy-start | bytes 196
  81.4 6.4 %copy-start.10 = (pred[32,2]{0,1:T(4,128)(4,1)S(1)}, pred[32,2]{0,1:T(4,128)(4,1)}, u32[]{:S(2)}) copy-start(pred[32,2]{0,1:T(4,128)(4,1)} %get-tuple-element.11) | copy-start | bytes 196
  89.8 7.8 %collective-permute-start.1 = (bf16[32,64,16]{1,2,0:T(8,128)(2,1)}, bf16[32,64,16]{1,2,0:T(8,128)(2,1)S(1)}, u32[]{:S(2)}, u32[]{:S(2)}) collective-permute-start(bf16[32,64,16]{1,2,0:T(8,128)(2,1)} %collective-permute-done), channel_id=1, source_target_pairs={{0,8},{8,16},{16,24},{24,0},{1,9},{9,17},{17,25},{25,1},{2,10},{10... | collective-permute-start | bytes 196616 | tf_op jit(solution)/shard_map/ppermute | solution.py:85
  97.6 7.2 %collective-permute-start.2 = (bf16[32,64,16]{1,2,0:T(8,128)(2,1)S(1)}, bf16[32,64,16]{1,2,0:T(8,128)(2,1)S(1)}, u32[]{:S(2)}, u32[]{:S(2)}) collective-permute-start(bf16[32,64,16]{1,2,0:T(8,128)(2,1)S(1)} %collective-permute-done.1), channel_id=1, source_target_pairs={{0,8},{8,16},{16,24},{24,0},{1,9},{9,17},{17,25},{25,1},{2,10},{10... | collective-permute-start | bytes 196616 | tf_op jit(solution)/shard_map/ppermute | solution.py:85
  98.3 9.5 %copy-start.7 = (s32[1024]{0:T(1024)S(1)}, s32[1024]{0:T(1024)}, u32[]{:S(2)}) copy-start(s32[1024]{0:T(1024)} %pad_clamp_fusion.1) | copy-start | bytes 12292
  104.8 4.6 %copy-start.14 = (pred[4,8]{1,0:T(4,128)(4,1)S(1)}, pred[4,8]{1,0:T(4,128)(4,1)}, u32[]{:S(2)}) copy-start(pred[4,8]{1,0:T(4,128)(4,1)} %get-tuple-element.18) | copy-start | bytes 100
  104.8 4.6 %copy-start.15 = (pred[4,8]{1,0:T(4,128)(4,1)S(1)}, pred[4,8]{1,0:T(4,128)(4,1)}, u32[]{:S(2)}) copy-start(pred[4,8]{1,0:T(4,128)(4,1)} %get-tuple-element.19) | copy-start | bytes 100
  104.8 6.0 %copy-start.6 = (bf16[8,64,64]{2,1,0:T(8,128)(2,1)S(1)}, bf16[8,64,64]{2,1,0:T(8,128)(2,1)}, u32[]{:S(2)}) copy-start(bf16[8,64,64]{2,1,0:T(8,128)(2,1)} %param.21) | copy-start | bytes 196612
  104.8 10.7 %copy-start.2 = (bf16[32,256,64]{1,2,0:T(8,128)(2,1)S(1)}, bf16[32,256,64]{1,2,0:T(8,128)(2,1)}, u32[]{:S(2)}) copy-start(bf16[32,256,64]{1,2,0:T(8,128)(2,1)} %param.16) | copy-start | bytes 3145732
